TPU v7x, 32 devices: a whole 2x2x4 slice. The times are simulated.
32 devices in a mesh: gx: 4 (over x, core), gy: 4 (over z), gz: 2 (over y).
Axes of the slice: x: 2, y: 2, z: 4, core: 2. Of those that a mesh axis runs over, the one named last changes fastest.
Arguments:
- kappa: float32 [5, 5, 5, 4, 4, 128], P(None, None, None, 'gx', 'gy', 'gz'), may hold values from 0.2 to 5
- source: float32 [5, 5, 5, 4, 4, 128], P(None, None, None, 'gx', 'gy', 'gz'), may hold values from -24 to 24
Outputs:
- solution: float32 [16, 16, 512], P('gx', 'gy', 'gz')
- residual: float32 [16, 16, 512], P('gx', 'gy', 'gz')
All inputs are finite; a program needn't handle non-finite values.
Results may differ from a plain program's by a relative error of at most 0.0003.
Values sent between devices are 32-bit elements; how exact they have to be, the bound alone decides.
A program may use at most 64 MiB of HBM per device.

v0:
```python
import math
import jax
import jax.numpy as jnp
import numpy as np
from jax import lax
from jax.sharding import PartitionSpec as P

LEVELS = 3
relax_weight = 0.6


def extended(cells, sides, width):
    for axis, dim in sides:
        count = lax.axis_size(axis)
        ends = count - 1
        head = lax.slice_in_dim(cells, 0, width, axis=dim)
        tail = lax.slice_in_dim(cells, cells.shape[dim] - width, cells.shape[dim], axis=dim)
        cells = jnp.concatenate(
            [
                lax.ppermute(tail, axis, [(i, (i + 1) % count) for i in range(ends)]),
                cells,
                lax.ppermute(head, axis, [((i + 1) % count, i) for i in range(ends)]),
            ],
            axis=dim,
        )
    return cells


def gll_tables():
    points = np.array([-1.0, -math.sqrt(3.0 / 7.0), 0.0, math.sqrt(3.0 / 7.0), 1.0])
    quad_weights = np.array([0.1, 49.0 / 90.0, 32.0 / 45.0, 49.0 / 90.0, 0.1])
    bary = np.array(
        [np.prod([points[i] - points[k] for k in range(5) if k != i]) for i in range(5)]
    )
    deriv = np.zeros((5, 5))
    for i in range(5):
        for j in range(5):
            if i != j:
                deriv[i, j] = bary[i] / (bary[j] * (points[i] - points[j]))
    for i in range(5):
        deriv[i, i] = -np.sum(deriv[i])
    return (
        jnp.asarray(points, jnp.float32),
        jnp.asarray(quad_weights, jnp.float32),
        jnp.asarray(deriv, jnp.float32),
    )


def split_first(values):
    count = (values.shape[0] - 1) // 4
    lower = jnp.swapaxes(values[:-1].reshape((count, 4) + values.shape[1:]), 0, 1)
    return jnp.concatenate([lower, values[4::4][None]], axis=0)


def merge_first(block):
    count = block.shape[1]
    rest = block.shape[2:]
    lower = jnp.swapaxes(block[:4], 0, 1).reshape((4 * count,) + rest)
    tail = jnp.concatenate([jnp.zeros((count, 3) + rest, block.dtype), block[4][:, None]], axis=1)
    tail = tail.reshape((4 * count,) + rest)
    spare = [(0, 0)] * len(rest)
    return jnp.pad(lower, [(0, 1)] + spare) + jnp.pad(tail, [(1, 0)] + spare)


def element_view(field):
    element_portion = split_first(field)
    element_portion = split_first(jnp.moveaxis(element_portion, 2, 0))
    element_portion = split_first(jnp.moveaxis(element_portion, 4, 0))
    return jnp.transpose(element_portion, (4, 2, 0, 5, 3, 1))


def node_sum(block):
    element_portion = jnp.transpose(block, (2, 5, 1, 4, 0, 3))
    element_portion = jnp.moveaxis(merge_first(element_portion), 0, 4)
    element_portion = jnp.moveaxis(merge_first(element_portion), 0, 2)
    return merge_first(element_portion)


def stiffness_terms(field, weighted, deriv):
    highest = lax.Precision.HIGHEST
    local = element_view(field)
    grad_x = jnp.einsum("ia,abcxyz->ibcxyz", deriv, local, precision=highest)
    grad_y = jnp.einsum("jb,abcxyz->ajcxyz", deriv, local, precision=highest)
    grad_z = jnp.einsum("kc,abcxyz->abkxyz", deriv, local, precision=highest)
    back = jnp.einsum("ia,ibcxyz->abcxyz", deriv, weighted * grad_x, precision=highest)
    back = back + jnp.einsum("jb,ajcxyz->abcxyz", deriv, weighted * grad_y, precision=highest)
    back = back + jnp.einsum("kc,abkxyz->abcxyz", deriv, weighted * grad_z, precision=highest)
    return node_sum(back)


def mass_pair(paired, width):
    return jnp.stack(
        [width / 6.0 * (2.0 * paired[0] + paired[1]), width / 6.0 * (paired[0] + 2.0 * paired[1])]
    )


def stiff_pair(paired, width):
    slope = (paired[0] - paired[1]) / width
    return jnp.stack([slope, -slope])


def lor_terms(field, coeff, spacing):
    width_x, width_y, width_z = spacing
    zpairs = jnp.stack([field[:, :, :-1], field[:, :, 1:]])
    zmass = mass_pair(zpairs, width_z)
    stiffness_along_z = stiff_pair(zpairs, width_z)
    ymass = jnp.stack([zmass[:, :, :-1], zmass[:, :, 1:]])
    ystiff = jnp.stack([stiffness_along_z[:, :, :-1], stiffness_along_z[:, :, 1:]])
    column_y = width_y[:, None]
    first = mass_pair(ymass, column_y)
    second = stiff_pair(ymass, column_y) + mass_pair(ystiff, column_y)
    column_x = width_x[:, None, None]
    xfirst = jnp.stack([first[:, :, :-1], first[:, :, 1:]])
    xsecond = jnp.stack([second[:, :, :-1], second[:, :, 1:]])
    cells = (stiff_pair(xfirst, column_x) + mass_pair(xsecond, column_x)) * coeff
    total = jnp.zeros(field.shape, jnp.float32)
    for a in range(2):
        for b in range(2):
            for c in range(2):
                total = total + jnp.pad(cells[a, b, c], ((a, 1 - a), (b, 1 - b), (c, 1 - c)))
    return total


def lor_diagonal(coeff, spacing):
    width_x = spacing[0][:, None, None]
    width_y = spacing[1][None, :, None]
    width_z = spacing[2][None, None, :]
    cells = coeff * (
        width_y * width_z / (9.0 * width_x)
        + width_x * width_z / (9.0 * width_y)
        + width_x * width_y / (9.0 * width_z)
    )
    shape = tuple((n + 1 for n in coeff.shape))
    total = jnp.zeros(shape, jnp.float32)
    for a in range(2):
        for b in range(2):
            for c in range(2):
                total = total + jnp.pad(cells, ((a, 1 - a), (b, 1 - b), (c, 1 - c)))
    return total


def subcell_coefficient(kappa):
    averaged = 0.5 * (kappa[:-1] + kappa[1:])
    averaged = 0.5 * (averaged[:, :-1] + averaged[:, 1:])
    averaged = 0.5 * (averaged[:, :, :-1] + averaged[:, :, 1:])
    count_x, count_y, count_z = averaged.shape[3:]
    return jnp.transpose(averaged, (3, 0, 4, 1, 5, 2)).reshape(
        4 * count_x, 4 * count_y, 4 * count_z
    )


def coarsen(coeff):
    nx, ny, nz = coeff.shape
    return jnp.mean(coeff.reshape(nx // 2, 2, ny // 2, 2, nz // 2, 2), axis=(1, 3, 5))


def interp_weights(width):
    paired = width.reshape(-1, 2)
    span = paired[:, 0] + paired[:, 1]
    return (paired[:, 1] / span, paired[:, 0] / span)


def prolong_first(coarse, left, right):
    shape = (-1,) + (1,) * (coarse.ndim - 1)
    middle = left.reshape(shape) * coarse[:-1] + right.reshape(shape) * coarse[1:]
    woven = jnp.stack([coarse[:-1], middle], axis=1).reshape(
        (2 * (coarse.shape[0] - 1),) + coarse.shape[1:]
    )
    return jnp.concatenate([woven, coarse[-1:]], axis=0)


def restrict_first(fine, left, right):
    shape = (-1,) + (1,) * (fine.ndim - 1)
    middle = fine[1::2]
    spare = [(0, 0)] * (fine.ndim - 1)
    return (
        fine[0::2]
        + jnp.pad(left.reshape(shape) * middle, [(0, 1)] + spare)
        + jnp.pad(right.reshape(shape) * middle, [(1, 0)] + spare)
    )


def prolong(coarse, weight_sets):
    for axis in range(3):
        left, right = weight_sets[axis]
        coarse = jnp.moveaxis(prolong_first(jnp.moveaxis(coarse, axis, 0), left, right), 0, axis)
    return coarse


def restrict(fine, weight_sets):
    for axis in range(3):
        left, right = weight_sets[axis]
        fine = jnp.moveaxis(restrict_first(jnp.moveaxis(fine, axis, 0), left, right), 0, axis)
    return fine


def collapse_leading(padded):
    inner = padded[1:-1]
    head = inner[0] + padded[0]
    tail = inner[-1] + padded[-1]
    return jnp.concatenate([head[None], inner[1:-1], tail[None]], axis=0)


def fold_axis(padded, axis):
    return jnp.moveaxis(collapse_leading(jnp.moveaxis(padded, axis, 0)), 0, axis)


def assemble(partial_value):
    padded = extended(partial_value, (("gx", 0), ("gy", 1), ("gz", 2)), 1)
    return fold_axis(fold_axis(fold_axis(padded, 0), 1), 2)


def side_mask(cells, position, devices):
    index = position * cells + jnp.arange(cells + 1)
    return ((index > 0) & (index < cells * devices)).astype(jnp.float32)


def block_mask(shape):
    mask_x = side_mask(shape[0], lax.axis_index("gx"), lax.axis_size("gx"))
    mask_y = side_mask(shape[1], lax.axis_index("gy"), lax.axis_size("gy"))
    mask_z = side_mask(shape[2], lax.axis_index("gz"), lax.axis_size("gz"))
    return mask_x[:, None, None] * mask_y[None, :, None] * mask_z[None, None, :]


def owned_mask(shape):
    sides = [(jnp.arange(n + 1) >= 1).astype(jnp.float32) for n in shape]
    return sides[0][:, None, None] * sides[1][None, :, None] * sides[2][None, None, :]


def cycle(level, forcing, levels):
    coeff, spacing, diag, mask, weight_sets, owned = levels[level]
    guess = relax_weight * forcing / diag
    if level == LEVELS - 1:
        guess = (
            guess
            + relax_weight * (forcing - mask * assemble(lor_terms(guess, coeff, spacing))) / diag
        )
        return guess
    defect = forcing * owned - lor_terms(guess, coeff, spacing)
    coarse = levels[level + 1][3] * assemble(restrict(defect, weight_sets))
    guess = guess + prolong(cycle(level + 1, coarse, levels), weight_sets)
    return (
        guess + relax_weight * (forcing - mask * assemble(lor_terms(guess, coeff, spacing))) / diag
    )


def inner_pair(resid, precond, image):
    local_rho = jnp.sum(resid[1:, 1:, 1:] * precond[1:, 1:, 1:])
    local_curv = jnp.sum(precond[1:, 1:, 1:] * image[1:, 1:, 1:])
    return lax.psum((local_rho, local_curv), ("gx", "gy", "gz"))


def body(kappa, source):
    points, quad_weights, deriv = gll_tables()
    cube = (
        quad_weights[:, None, None] * quad_weights[None, :, None] * quad_weights[None, None, :]
    ).reshape(5, 5, 5, 1, 1, 1)
    weighted = kappa * cube
    counts = kappa.shape[3:]
    finest_mask = block_mask([4 * c for c in counts])
    rhs = finest_mask * assemble(node_sum(cube * source))
    gaps = points[1:] - points[:-1]
    spacing = [jnp.tile(gaps, c) for c in counts]
    coeff = subcell_coefficient(kappa)
    levels = []
    for level in range(LEVELS):
        weight_sets = [interp_weights(h) for h in spacing] if level < LEVELS - 1 else None
        diag = assemble(lor_diagonal(coeff, spacing))
        levels.append(
            (coeff, spacing, diag, block_mask(coeff.shape), weight_sets, owned_mask(coeff.shape))
        )
        if level < LEVELS - 1:
            coeff = coarsen(coeff)
            spacing = [h.reshape(-1, 2).sum(axis=1) for h in spacing]

    def operator(field):
        return finest_mask * assemble(stiffness_terms(field, weighted, deriv))

    resid = rhs
    precond = cycle(0, resid, levels)
    image = operator(precond)
    rho_old, curv = inner_pair(resid, precond, image)
    alpha = rho_old / curv
    direction, along = (precond, image)
    iterate = alpha * direction
    resid = resid - alpha * along
    precond = cycle(0, resid, levels)
    image = operator(precond)
    rho_new, curv = inner_pair(resid, precond, image)
    ratio = rho_new / rho_old
    alpha = rho_new / (curv - ratio * rho_new / alpha)
    direction = precond + ratio * direction
    along = image + ratio * along
    iterate = iterate + alpha * direction
    resid = resid - alpha * along
    return (iterate[1:, 1:, 1:], resid[1:, 1:, 1:])


def solution(mesh):
    placed = (P(None, None, None, "gx", "gy", "gz"), P(None, None, None, "gx", "gy", "gz"))
    return jax.shard_map(
        body,
        mesh=mesh,
        in_specs=placed,
        out_specs=(P("gx", "gy", "gz"), P("gx", "gy", "gz")),
        check_vma=False,
    )
```

profile of v0, /device:TPU:14, one launch (start us, length us, event | category | flops | bytes accessed | tf_op | source)
XLA Modules:
  0.0 476.9 jit_solution(2688961487254693226)
XLA Ops:
  36.4 4.5 collective-permute-start.35
  51.3 4.5 collective-permute-start.23
  59.9 3.9 collective-permute-start.9
  71.1 4.5 collective-permute-start.11
  77.0 4.5 collective-permute-start.5
  103.3 4.5 collective-permute-start.17
  119.3 3.9 collective-permute-start.27
  126.2 4.5 collective-permute-start.29
  148.5 4.5 collective-permute-start.41
  171.4 4.5 collective-permute-start.47
  190.9 3.9 collective-permute-start.51
  197.8 4.5 collective-permute-start.53
  221.2 3.9 collective-permute-start.57
  228.1 4.5 collective-permute-start.59
  235.6 42.7 %all-reduce.156 = (f32[]{:T(128)}, f32[]{:T(128)}) all-reduce(f32[]{:T(128)} %get-tuple-element.13, f32[]{:T(128)} %get-tuple-element.12), channel_id=1, replica_groups=mesh['gx'=4,'gy'=4,'gz'=2] {'gx','gy','gz'}, use_global_device_ids=true, to_apply=%region_6.7 | all-reduce | flops 2 | bytes 16 | tf_op jit(solution)/shard_map/psum | solution.py:250
  297.8 4.5 collective-permute-start.65
  320.7 4.5 collective-permute-start.71
  343.0 4.5 collective-permute-start.77
  366.0 4.8 collective-permute-start.83
  384.1 3.9 collective-permute-start.87
  391.0 4.5 collective-permute-start.89
  413.7 3.9 collective-permute-start.93
  420.6 4.5 collective-permute-start.95
  428.2 42.7 %all-reduce.155 = (f32[]{:T(128)}, f32[]{:T(128)}) all-reduce(f32[]{:T(128)} %get-tuple-element.11, f32[]{:T(128)} %get-tuple-element.10), channel_id=1, replica_groups=mesh['gx'=4,'gy'=4,'gz'=2] {'gx','gy','gz'}, use_global_device_ids=true, to_apply=%region_10.11 | all-reduce | flops 2 | bytes 16 | tf_op jit(solution)/shard_map/psum | solution.py:250
  (754 shorter events, 284.3 us)
Async XLA Ops:
  3.1 54.8 %collective-permute-start.6 = (f32[1,5,257]{2,1,0:T(8,128)S(1)}, f32[1,5,257]{2,1,0:T(8,128)S(1)}, u32[]{:S(2)}, u32[]{:S(2)}) collective-permute-start(f32[1,5,257]{2,1,0:T(8,128)S(1)} %get-tuple-element.233), channel_id=1, source_target_pairs={{0,8},{8,16},{16,24},{1,9},{9,17},{17,25},{2,10},{10,18},{18,26},{... | collective-permute-start | bytes 15428 | tf_op jit(solution)/shard_map/ppermute | solution.py:20
  5.1 52.9 %collective-permute-start.7 = (f32[1,5,257]{2,1,0:T(8,128)S(1)}, f32[1,5,257]{2,1,0:T(8,128)S(1)}, u32[]{:S(2)}, u32[]{:S(2)}) collective-permute-start(f32[1,5,257]{2,1,0:T(8,128)S(1)} %get-tuple-element.234), channel_id=1, source_target_pairs={{8,0},{16,8},{24,16},{9,1},{17,9},{25,17},{10,2},{18,10},{26,18},{... | collective-permute-start | bytes 15428 | tf_op jit(solution)/shard_map/ppermute | solution.py:22
  9.2 16.8 %collective-permute-start.18 = (f32[1,3,129]{2,1,0:T(4,128)S(1)}, f32[1,3,129]{2,1,0:T(4,128)S(1)}, u32[]{:S(2)}, u32[]{:S(2)}) collective-permute-start(f32[1,3,129]{2,1,0:T(4,128)S(1)} %get-tuple-element.387), channel_id=1, source_target_pairs={{0,8},{8,16},{16,24},{1,9},{9,17},{17,25},{2,10},{10,18},{18,26},{... | collective-permute-start | bytes 4652 | tf_op jit(solution)/shard_map/ppermute | solution.py:20
  11.5 10.1 %collective-permute-start.30 = (f32[1,2,65]{2,1,0:T(2,128)S(1)}, f32[1,2,65]{2,1,0:T(2,128)S(1)}, u32[]{:S(2)}, u32[]{:S(2)}) collective-permute-start(f32[1,2,65]{2,1,0:T(2,128)S(1)} %get-tuple-element.509), channel_id=1, source_target_pairs={{0,8},{8,16},{16,24},{1,9},{9,17},{17,25},{2,10},{10,18},{18,26},{... | collective-permute-start | bytes 1568 | tf_op jit(solution)/shard_map/ppermute | solution.py:20
  13.4 10.6 %collective-permute-start.31 = (f32[1,2,65]{2,1,0:T(2,128)S(1)}, f32[1,2,65]{2,1,0:T(2,128)S(1)}, u32[]{:S(2)}, u32[]{:S(2)}) collective-permute-start(f32[1,2,65]{2,1,0:T(2,128)S(1)} %get-tuple-element.510), channel_id=1, source_target_pairs={{8,0},{16,8},{24,16},{9,1},{17,9},{25,17},{10,2},{18,10},{26,18},{... | collective-permute-start | bytes 1568 | tf_op jit(solution)/shard_map/ppermute | solution.py:22
  21.6 7.9 %collective-permute-start.19 = (f32[1,3,129]{2,1,0:T(4,128)S(1)}, f32[1,3,129]{2,1,0:T(4,128)S(1)}, u32[]{:S(2)}, u32[]{:S(2)}) collective-permute-start(f32[1,3,129]{2,1,0:T(4,128)S(1)} %get-tuple-element.388), channel_id=1, source_target_pairs={{8,0},{16,8},{24,16},{9,1},{17,9},{25,17},{10,2},{18,10},{26,18},{... | collective-permute-start | bytes 4652 | tf_op jit(solution)/shard_map/ppermute | solution.py:22
  24.0 39.8 %collective-permute-start = (f32[1,5,257]{2,1,0:T(8,128)S(1)}, f32[1,5,257]{2,1,0:T(8,128)S(1)}, u32[]{:S(2)}, u32[]{:S(2)}) collective-permute-start(f32[1,5,257]{2,1,0:T(8,128)S(1)} %get-tuple-element.131), channel_id=1, source_target_pairs={{0,8},{8,16},{16,24},{1,9},{9,17},{17,25},{2,10},{10,18},{18,26},{... | collective-permute-start | bytes 15428 | tf_op jit(solution)/shard_map/ppermute | solution.py:20
  36.4 8.1 %collective-permute-start.35 = (f32[4,4,1]{2,1,0:T(4,128)S(1)}, f32[4,4,1]{2,1,0:T(4,128)S(1)}, u32[]{:S(2)}, u32[]{:S(2)}) collective-permute-start(f32[4,4,1]{2,1,0:T(4,128)S(1)} %get-tuple-element.412), channel_id=1, source_target_pairs={{1,0},{3,2},{5,4},{7,6},{9,8},{11,10},{13,12},{15,14},{17,16},{19,... | collective-permute-start | bytes 200 | tf_op jit(solution)/shard_map/ppermute | solution.py:22
  51.3 6.5 %collective-permute-start.23 = (f32[5,5,1]{2,1,0:T(8,128)S(1)}, f32[5,5,1]{2,1,0:T(8,128)S(1)}, u32[]{:S(2)}, u32[]{:S(2)}) collective-permute-start(f32[5,5,1]{2,1,0:T(8,128)S(1)} %get-tuple-element.258), channel_id=1, source_target_pairs={{1,0},{3,2},{5,4},{7,6},{9,8},{11,10},{13,12},{15,14},{17,16},{19,... | collective-permute-start | bytes 308 | tf_op jit(solution)/shard_map/ppermute | solution.py:22
  55.8 8.0 %collective-permute-start.1 = (f32[1,5,257]{2,1,0:T(8,128)S(1)}, f32[1,5,257]{2,1,0:T(8,128)S(1)}, u32[]{:S(2)}, u32[]{:S(2)}) collective-permute-start(f32[1,5,257]{2,1,0:T(8,128)S(1)} %get-tuple-element.132), channel_id=1, source_target_pairs={{8,0},{16,8},{24,16},{9,1},{17,9},{25,17},{10,2},{18,10},{26,18},{... | collective-permute-start | bytes 15428 | tf_op jit(solution)/shard_map/ppermute | solution.py:22
  58.0 11.8 %collective-permute-start.8 = (f32[7,1,257]{2,1,0:T(1,128)S(1)}, f32[7,1,257]{2,1,0:T(1,128)S(1)}, u32[]{:S(2)}, u32[]{:S(2)}) collective-permute-start(f32[7,1,257]{2,1,0:T(1,128)S(1)} %get-tuple-element.143), channel_id=1, source_target_pairs={{0,2},{2,4},{4,6},{1,3},{3,5},{5,7},{8,10},{10,12},{12,14},{9,11},... | collective-permute-start | bytes 21596 | tf_op jit(solution)/shard_map/ppermute | solution.py:20
  59.9 9.8 %collective-permute-start.9 = (f32[7,1,257]{2,1,0:T(1,128)S(1)}, f32[7,1,257]{2,1,0:T(1,128)S(1)}, u32[]{:S(2)}, u32[]{:S(2)}) collective-permute-start(f32[7,1,257]{2,1,0:T(1,128)S(1)} %get-tuple-element.144), channel_id=1, source_target_pairs={{2,0},{4,2},{6,4},{3,1},{5,3},{7,5},{10,8},{12,10},{14,12},{11,9},... | collective-permute-start | bytes 21596 | tf_op jit(solution)/shard_map/ppermute | solution.py:22
  63.9 11.8 %collective-permute-start.2 = (f32[7,1,257]{2,1,0:T(1,128)S(1)}, f32[7,1,257]{2,1,0:T(1,128)S(1)}, u32[]{:S(2)}, u32[]{:S(2)}) collective-permute-start(f32[7,1,257]{2,1,0:T(1,128)S(1)} %get-tuple-element.141), channel_id=1, source_target_pairs={{0,2},{2,4},{4,6},{1,3},{3,5},{5,7},{8,10},{10,12},{12,14},{9,11},... | collective-permute-start | bytes 21596 | tf_op jit(solution)/shard_map/ppermute | solution.py:20
  65.8 9.8 %collective-permute-start.3 = (f32[7,1,257]{2,1,0:T(1,128)S(1)}, f32[7,1,257]{2,1,0:T(1,128)S(1)}, u32[]{:S(2)}, u32[]{:S(2)}) collective-permute-start(f32[7,1,257]{2,1,0:T(1,128)S(1)} %get-tuple-element.142), channel_id=1, source_target_pairs={{2,0},{4,2},{6,4},{3,1},{5,3},{7,5},{10,8},{12,10},{14,12},{11,9},... | collective-permute-start | bytes 21596 | tf_op jit(solution)/shard_map/ppermute | solution.py:22
  69.8 11.8 %collective-permute-start.10 = (f32[7,7,1]{2,1,0:T(8,128)S(1)}, f32[7,7,1]{2,1,0:T(8,128)S(1)}, u32[]{:S(2)}, u32[]{:S(2)}) collective-permute-start(f32[7,7,1]{2,1,0:T(8,128)S(1)} %get-tuple-element.125), channel_id=1, source_target_pairs={{0,1},{2,3},{4,5},{6,7},{8,9},{10,11},{12,13},{14,15},{16,17},{18,... | collective-permute-start | bytes 596 | tf_op jit(solution)/shard_map/ppermute | solution.py:20
  71.1 10.5 %collective-permute-start.11 = (f32[7,7,1]{2,1,0:T(8,128)S(1)}, f32[7,7,1]{2,1,0:T(8,128)S(1)}, u32[]{:S(2)}, u32[]{:S(2)}) collective-permute-start(f32[7,7,1]{2,1,0:T(8,128)S(1)} %get-tuple-element.126), channel_id=1, source_target_pairs={{1,0},{3,2},{5,4},{7,6},{9,8},{11,10},{13,12},{15,14},{17,16},{19,... | collective-permute-start | bytes 596 | tf_op jit(solution)/shard_map/ppermute | solution.py:22
  75.7 6.3 %collective-permute-start.4 = (f32[7,7,1]{2,1,0:T(8,128)S(1)}, f32[7,7,1]{2,1,0:T(8,128)S(1)}, u32[]{:S(2)}, u32[]{:S(2)}) collective-permute-start(f32[7,7,1]{2,1,0:T(8,128)S(1)} %get-tuple-element.123), channel_id=1, source_target_pairs={{0,1},{2,3},{4,5},{6,7},{8,9},{10,11},{12,13},{14,15},{16,17},{18,... | collective-permute-start | bytes 596 | tf_op jit(solution)/shard_map/ppermute | solution.py:20
  77.0 6.1 %collective-permute-start.5 = (f32[7,7,1]{2,1,0:T(8,128)S(1)}, f32[7,7,1]{2,1,0:T(8,128)S(1)}, u32[]{:S(2)}, u32[]{:S(2)}) collective-permute-start(f32[7,7,1]{2,1,0:T(8,128)S(1)} %get-tuple-element.124), channel_id=1, source_target_pairs={{1,0},{3,2},{5,4},{7,6},{9,8},{11,10},{13,12},{15,14},{17,16},{19,... | collective-permute-start | bytes 596 | tf_op jit(solution)/shard_map/ppermute | solution.py:22
  103.3 6.0 %collective-permute-start.17 = (f32[5,5,1]{2,1,0:T(8,128)S(1)}, f32[5,5,1]{2,1,0:T(8,128)S(1)}, u32[]{:S(2)}, u32[]{:S(2)}) collective-permute-start(f32[5,5,1]{2,1,0:T(8,128)S(1)} %get-tuple-element.263), channel_id=1, source_target_pairs={{1,0},{3,2},{5,4},{7,6},{9,8},{11,10},{13,12},{15,14},{17,16},{19,... | collective-permute-start | bytes 308 | tf_op jit(solution)/shard_map/ppermute | solution.py:22
  197.8 6.1 %collective-permute-start.53 = (f32[7,7,1]{2,1,0:T(8,128)S(1)}, f32[7,7,1]{2,1,0:T(8,128)S(1)}, u32[]{:S(2)}, u32[]{:S(2)}) collective-permute-start(f32[7,7,1]{2,1,0:T(8,128)S(1)} %get-tuple-element.122), channel_id=1, source_target_pairs={{1,0},{3,2},{5,4},{7,6},{9,8},{11,10},{13,12},{15,14},{17,16},{19,... | collective-permute-start | bytes 596 | tf_op jit(solution)/shard_map/ppermute | solution.py:22
  228.1 6.1 %collective-permute-start.59 = (f32[7,7,1]{2,1,0:T(8,128)S(1)}, f32[7,7,1]{2,1,0:T(8,128)S(1)}, u32[]{:S(2)}, u32[]{:S(2)}) collective-permute-start(f32[7,7,1]{2,1,0:T(8,128)S(1)} %get-tuple-element.120), channel_id=1, source_target_pairs={{1,0},{3,2},{5,4},{7,6},{9,8},{11,10},{13,12},{15,14},{17,16},{19,... | collective-permute-start | bytes 596 | tf_op jit(solution)/shard_map/ppermute | solution.py:22
  364.7 6.1 %collective-permute-start.82 = (f32[5,5,1]{2,1,0:T(8,128)S(1)}, f32[5,5,1]{2,1,0:T(8,128)S(1)}, u32[]{:S(2)}, u32[]{:S(2)}) collective-permute-start(f32[5,5,1]{2,1,0:T(8,128)S(1)} %get-tuple-element.240), channel_id=1, source_target_pairs={{0,1},{2,3},{4,5},{6,7},{8,9},{10,11},{12,13},{14,15},{16,17},{18,... | collective-permute-start | bytes 308 | tf_op jit(solution)/shard_map/ppermute | solution.py:20
  391.0 6.1 %collective-permute-start.89 = (f32[7,7,1]{2,1,0:T(8,128)S(1)}, f32[7,7,1]{2,1,0:T(8,128)S(1)}, u32[]{:S(2)}, u32[]{:S(2)}) collective-permute-start(f32[7,7,1]{2,1,0:T(8,128)S(1)} %get-tuple-element.118), channel_id=1, source_target_pairs={{1,0},{3,2},{5,4},{7,6},{9,8},{11,10},{13,12},{15,14},{17,16},{19,... | collective-permute-start | bytes 596 | tf_op jit(solution)/shard_map/ppermute | solution.py:22
  420.6 6.1 %collective-permute-start.95 = (f32[7,7,1]{2,1,0:T(8,128)S(1)}, f32[7,7,1]{2,1,0:T(8,128)S(1)}, u32[]{:S(2)}, u32[]{:S(2)}) collective-permute-start(f32[7,7,1]{2,1,0:T(8,128)S(1)} %get-tuple-element.116), channel_id=1, source_target_pairs={{1,0},{3,2},{5,4},{7,6},{9,8},{11,10},{13,12},{15,14},{17,16},{19,... | collective-permute-start | bytes 596 | tf_op jit(solution)/shard_map/ppermute | solution.py:22
  (93 other events, 424.9 us)
where the time goes:
time: 480 us; the launch traced here: 477 us
  starting transfers between devices  273 us (57%)
  blocking collectives  85.4 us (18%)
  waiting for transfers between devices  59.4 us (12%)
  local copies, waits for them, and re-layouts  27.5 us (6%)
  other arithmetic  17.6 us (4%)
  between operations  10.7 us (2%)
    ppermute x48, starting transfers between devices, extended(): lax.ppermute(head, axis, [((i + 1) % count, i) for i in range(ends)])  187 us
    ppermute x48, starting transfers between devices, extended(): lax.ppermute(tail, axis, [(i, (i + 1) % count) for i in range(ends)])  85.8 us
    psum x2, blocking collectives, inner_pair(): return lax.psum((local_rho, local_curv), ('gx', 'gy', 'gz'))  85.4 us
    ppermute x48, waiting for transfers between devices, extended(): lax.ppermute(head, axis, [((i + 1) % count, i) for i in range(ends)])  59.3 us
  transfers between devices with their start and end apart: 96, of which 39 were waited for; matrix products, arithmetic and copies ran while one was open for 1% of the time, Pallas kernels for 0%

commit v1 on v0

--- a/solution.py
+++ b/solution.py
@@ -7,6 +7,10 @@
 
 LEVELS = 3
 relax_weight = 0.6
+
+
+def keys_show(obj):
+    return lax.psum(lax.psum(obj, ("gy", "gz")), "gx")
 
 
 def extended(cells, sides, width):
@@ -247,7 +251,7 @@
 def inner_pair(resid, precond, image):
     local_rho = jnp.sum(resid[1:, 1:, 1:] * precond[1:, 1:, 1:])
     local_curv = jnp.sum(precond[1:, 1:, 1:] * image[1:, 1:, 1:])
-    return lax.psum((local_rho, local_curv), ("gx", "gy", "gz"))
+    return keys_show((local_rho, local_curv))
 
 
 def body(kappa, source):

time: 480 us -> 450 us (0.938)
  blocking collectives: 85.4 us -> 50.5 us
    psum x2 -> x4, blocking collectives: 85.4 us -> 50.5 us  [keys_show(): return lax.psum(lax.psum(obj, ('gy', 'gz')), 'gx')]
where the time goes in v1:
time: 450 us; the launch traced here: 444 us
  starting transfers between devices  274 us (61%)
  waiting for transfers between devices  61.1 us (14%)
  blocking collectives  50.5 us (11%)
  local copies, waits for them, and re-layouts  27.5 us (6%)
  other arithmetic  17.6 us (4%)
  between operations  10.8 us (2%)
    ppermute x48, starting transfers between devices, extended(): lax.ppermute(head, axis, [((i + 1) % count, i) for i in range(ends)])  187 us
    ppermute x48, starting transfers between devices, extended(): lax.ppermute(tail, axis, [(i, (i + 1) % count) for i in range(ends)])  87.2 us
    ppermute x48, waiting for transfers between devices, extended(): lax.ppermute(head, axis, [((i + 1) % count, i) for i in range(ends)])  61 us
    psum x4, blocking collectives, keys_show(): return lax.psum(lax.psum(obj, ('gy', 'gz')), 'gx')  50.5 us
  transfers between devices with their start and end apart: 96, of which 39 were waited for; matrix products, arithmetic and copies ran while one was open for 1% of the time, Pallas kernels for 0%

profile of v1, /device:TPU:14, one launch (start us, length us, event | category | flops | bytes accessed | tf_op | source)
XLA Modules:
  0.0 444.3 jit_solution(137154279380583342)
XLA Ops:
  36.4 4.5 %collective-permute-start.35 = (f32[4,4,1]{2,1,0:T(4,128)S(1)}, f32[4,4,1]{2,1,0:T(4,128)S(1)}, u32[]{:S(2)}, u32[]{:S(2)}) collective-permute-start(f32[4,4,1]{2,1,0:T(4,128)S(1)} %get-tuple-element.416), channel_id=1, source_target_pairs={{1,0},{3,2},{5,4},{7,6},{9,8},{11,10},{13,12},{15,14},{17,16},{19,... | collective-permute-start | bytes 200 | tf_op jit(solution)/shard_map/ppermute | solution.py:26
  51.3 4.5 %collective-permute-start.23 = (f32[5,5,1]{2,1,0:T(8,128)S(1)}, f32[5,5,1]{2,1,0:T(8,128)S(1)}, u32[]{:S(2)}, u32[]{:S(2)}) collective-permute-start(f32[5,5,1]{2,1,0:T(8,128)S(1)} %get-tuple-element.262), channel_id=1, source_target_pairs={{1,0},{3,2},{5,4},{7,6},{9,8},{11,10},{13,12},{15,14},{17,16},{19,... | collective-permute-start | bytes 308 | tf_op jit(solution)/shard_map/ppermute | solution.py:26
  59.9 3.9 collective-permute-start.9
  71.1 4.5 %collective-permute-start.11 = (f32[7,7,1]{2,1,0:T(8,128)S(1)}, f32[7,7,1]{2,1,0:T(8,128)S(1)}, u32[]{:S(2)}, u32[]{:S(2)}) collective-permute-start(f32[7,7,1]{2,1,0:T(8,128)S(1)} %get-tuple-element.130), channel_id=1, source_target_pairs={{1,0},{3,2},{5,4},{7,6},{9,8},{11,10},{13,12},{15,14},{17,16},{19,... | collective-permute-start | bytes 596 | tf_op jit(solution)/shard_map/ppermute | solution.py:26
  77.0 4.5 %collective-permute-start.5 = (f32[7,7,1]{2,1,0:T(8,128)S(1)}, f32[7,7,1]{2,1,0:T(8,128)S(1)}, u32[]{:S(2)}, u32[]{:S(2)}) collective-permute-start(f32[7,7,1]{2,1,0:T(8,128)S(1)} %get-tuple-element.128), channel_id=1, source_target_pairs={{1,0},{3,2},{5,4},{7,6},{9,8},{11,10},{13,12},{15,14},{17,16},{19,... | collective-permute-start | bytes 596 | tf_op jit(solution)/shard_map/ppermute | solution.py:26
  103.3 4.5 %collective-permute-start.17 = (f32[5,5,1]{2,1,0:T(8,128)S(1)}, f32[5,5,1]{2,1,0:T(8,128)S(1)}, u32[]{:S(2)}, u32[]{:S(2)}) collective-permute-start(f32[5,5,1]{2,1,0:T(8,128)S(1)} %get-tuple-element.267), channel_id=1, source_target_pairs={{1,0},{3,2},{5,4},{7,6},{9,8},{11,10},{13,12},{15,14},{17,16},{19,... | collective-permute-start | bytes 308 | tf_op jit(solution)/shard_map/ppermute | solution.py:26
  126.2 4.5 %collective-permute-start.29 = (f32[4,4,1]{2,1,0:T(4,128)S(1)}, f32[4,4,1]{2,1,0:T(4,128)S(1)}, u32[]{:S(2)}, u32[]{:S(2)}) collective-permute-start(f32[4,4,1]{2,1,0:T(4,128)S(1)} %get-tuple-element.420), channel_id=1, source_target_pairs={{1,0},{3,2},{5,4},{7,6},{9,8},{11,10},{13,12},{15,14},{17,16},{19,... | collective-permute-start | bytes 200 | tf_op jit(solution)/shard_map/ppermute | solution.py:26
  148.5 4.5 %collective-permute-start.41 = (f32[4,4,1]{2,1,0:T(4,128)S(1)}, f32[4,4,1]{2,1,0:T(4,128)S(1)}, u32[]{:S(2)}, u32[]{:S(2)}) collective-permute-start(f32[4,4,1]{2,1,0:T(4,128)S(1)} %get-tuple-element.412), channel_id=1, source_target_pairs={{1,0},{3,2},{5,4},{7,6},{9,8},{11,10},{13,12},{15,14},{17,16},{19,... | collective-permute-start | bytes 200 | tf_op jit(solution)/shard_map/ppermute | solution.py:26
  171.4 4.5 %collective-permute-start.47 = (f32[5,5,1]{2,1,0:T(8,128)S(1)}, f32[5,5,1]{2,1,0:T(8,128)S(1)}, u32[]{:S(2)}, u32[]{:S(2)}) collective-permute-start(f32[5,5,1]{2,1,0:T(8,128)S(1)} %get-tuple-element.257), channel_id=1, source_target_pairs={{1,0},{3,2},{5,4},{7,6},{9,8},{11,10},{13,12},{15,14},{17,16},{19,... | collective-permute-start | bytes 308 | tf_op jit(solution)/shard_map/ppermute | solution.py:26
  190.9 3.9 collective-permute-start.51
  197.8 4.5 %collective-permute-start.53 = (f32[7,7,1]{2,1,0:T(8,128)S(1)}, f32[7,7,1]{2,1,0:T(8,128)S(1)}, u32[]{:S(2)}, u32[]{:S(2)}) collective-permute-start(f32[7,7,1]{2,1,0:T(8,128)S(1)} %get-tuple-element.126), channel_id=1, source_target_pairs={{1,0},{3,2},{5,4},{7,6},{9,8},{11,10},{13,12},{15,14},{17,16},{19,... | collective-permute-start | bytes 596 | tf_op jit(solution)/shard_map/ppermute | solution.py:26
  228.1 4.5 %collective-permute-start.59 = (f32[7,7,1]{2,1,0:T(8,128)S(1)}, f32[7,7,1]{2,1,0:T(8,128)S(1)}, u32[]{:S(2)}, u32[]{:S(2)}) collective-permute-start(f32[7,7,1]{2,1,0:T(8,128)S(1)} %get-tuple-element.124), channel_id=1, source_target_pairs={{1,0},{3,2},{5,4},{7,6},{9,8},{11,10},{13,12},{15,14},{17,16},{19,... | collective-permute-start | bytes 596 | tf_op jit(solution)/shard_map/ppermute | solution.py:26
  235.6 18.8 %all-reduce.156 = (f32[]{:T(128)}, f32[]{:T(128)}) all-reduce(f32[]{:T(128)} %get-tuple-element.13, f32[]{:T(128)} %get-tuple-element.12), channel_id=1, replica_groups=mesh['gx'=4,'gy'=4,'gz'=2] {'gy','gz'}, use_global_device_ids=true, to_apply=%region_6.7 | all-reduce | flops 2 | bytes 16 | tf_op jit(solution)/shard_map/psum | solution.py:13
  254.4 6.4 %all-reduce.158 = (f32[]{:T(128)}, f32[]{:T(128)}) all-reduce(f32[]{:T(128)} %get-tuple-element.16, f32[]{:T(128)} %get-tuple-element.17), channel_id=1, replica_groups=mesh['gx'=4,'gy'=4,'gz'=2] {'gx'}, use_global_device_ids=true, to_apply=%region_7.8 | all-reduce | flops 2 | bytes 16 | tf_op jit(solution)/shard_map/psum | solution.py:13
  272.8 4.5 %collective-permute-start.63 = (f32[5,1,129]{2,1,0:T(1,128)S(1)}, f32[5,1,129]{2,1,0:T(1,128)S(1)}, u32[]{:S(2)}, u32[]{:S(2)}) collective-permute-start(f32[5,1,129]{2,1,0:T(1,128)S(1)} %get-tuple-element.288), channel_id=1, source_target_pairs={{2,0},{4,2},{6,4},{3,1},{5,3},{7,5},{10,8},{12,10},{14,12},{11,9},... | collective-permute-start | bytes 7748 | tf_op jit(solution)/shard_map/ppermute | solution.py:26
  280.5 4.5 %collective-permute-start.65 = (f32[5,5,1]{2,1,0:T(8,128)S(1)}, f32[5,5,1]{2,1,0:T(8,128)S(1)}, u32[]{:S(2)}, u32[]{:S(2)}) collective-permute-start(f32[5,5,1]{2,1,0:T(8,128)S(1)} %get-tuple-element.250), channel_id=1, source_target_pairs={{1,0},{3,2},{5,4},{7,6},{9,8},{11,10},{13,12},{15,14},{17,16},{19,... | collective-permute-start | bytes 308 | tf_op jit(solution)/shard_map/ppermute | solution.py:26
  294.7 3.9 collective-permute-start.68
  305.5 4.5 %collective-permute-start.71 = (f32[4,4,1]{2,1,0:T(4,128)S(1)}, f32[4,4,1]{2,1,0:T(4,128)S(1)}, u32[]{:S(2)}, u32[]{:S(2)}) collective-permute-start(f32[4,4,1]{2,1,0:T(4,128)S(1)} %get-tuple-element.408), channel_id=1, source_target_pairs={{1,0},{3,2},{5,4},{7,6},{9,8},{11,10},{13,12},{15,14},{17,16},{19,... | collective-permute-start | bytes 200 | tf_op jit(solution)/shard_map/ppermute | solution.py:26
  327.8 4.5 %collective-permute-start.77 = (f32[4,4,1]{2,1,0:T(4,128)S(1)}, f32[4,4,1]{2,1,0:T(4,128)S(1)}, u32[]{:S(2)}, u32[]{:S(2)}) collective-permute-start(f32[4,4,1]{2,1,0:T(4,128)S(1)} %get-tuple-element.404), channel_id=1, source_target_pairs={{1,0},{3,2},{5,4},{7,6},{9,8},{11,10},{13,12},{15,14},{17,16},{19,... | collective-permute-start | bytes 200 | tf_op jit(solution)/shard_map/ppermute | solution.py:26
  350.7 4.5 %collective-permute-start.83 = (f32[5,5,1]{2,1,0:T(8,128)S(1)}, f32[5,5,1]{2,1,0:T(8,128)S(1)}, u32[]{:S(2)}, u32[]{:S(2)}) collective-permute-start(f32[5,5,1]{2,1,0:T(8,128)S(1)} %get-tuple-element.245), channel_id=1, source_target_pairs={{1,0},{3,2},{5,4},{7,6},{9,8},{11,10},{13,12},{15,14},{17,16},{19,... | collective-permute-start | bytes 308 | tf_op jit(solution)/shard_map/ppermute | solution.py:26
  375.7 4.8 %collective-permute-start.89 = (f32[7,7,1]{2,1,0:T(8,128)S(1)}, f32[7,7,1]{2,1,0:T(8,128)S(1)}, u32[]{:S(2)}, u32[]{:S(2)}) collective-permute-start(f32[7,7,1]{2,1,0:T(8,128)S(1)} %get-tuple-element.122), channel_id=1, source_target_pairs={{1,0},{3,2},{5,4},{7,6},{9,8},{11,10},{13,12},{15,14},{17,16},{19,... | collective-permute-start | bytes 596 | tf_op jit(solution)/shard_map/ppermute | solution.py:26
  405.4 4.5 %collective-permute-start.95 = (f32[7,7,1]{2,1,0:T(8,128)S(1)}, f32[7,7,1]{2,1,0:T(8,128)S(1)}, u32[]{:S(2)}, u32[]{:S(2)}) collective-permute-start(f32[7,7,1]{2,1,0:T(8,128)S(1)} %get-tuple-element.120), channel_id=1, source_target_pairs={{1,0},{3,2},{5,4},{7,6},{9,8},{11,10},{13,12},{15,14},{17,16},{19,... | collective-permute-start | bytes 596 | tf_op jit(solution)/shard_map/ppermute | solution.py:26
  412.9 18.9 %all-reduce.155 = (f32[]{:T(128)}, f32[]{:T(128)}) all-reduce(f32[]{:T(128)} %get-tuple-element.11, f32[]{:T(128)} %get-tuple-element.10), channel_id=1, replica_groups=mesh['gx'=4,'gy'=4,'gz'=2] {'gy','gz'}, use_global_device_ids=true, to_apply=%region_12.13 | all-reduce | flops 2 | bytes 16 | tf_op jit(solution)/shard_map/psum | solution.py:13
  431.8 6.4 %all-reduce.157 = (f32[]{:T(128)}, f32[]{:T(128)}) all-reduce(f32[]{:T(128)} %get-tuple-element.14, f32[]{:T(128)} %get-tuple-element.15), channel_id=1, replica_groups=mesh['gx'=4,'gy'=4,'gz'=2] {'gx'}, use_global_device_ids=true, to_apply=%region_13.14 | all-reduce | flops 2 | bytes 16 | tf_op jit(solution)/shard_map/psum | solution.py:13
  (756 shorter events, 293.8 us)
Async XLA Ops:
  3.1 54.8 %collective-permute-start.6 = (f32[1,5,257]{2,1,0:T(8,128)S(1)}, f32[1,5,257]{2,1,0:T(8,128)S(1)}, u32[]{:S(2)}, u32[]{:S(2)}) collective-permute-start(f32[1,5,257]{2,1,0:T(8,128)S(1)} %get-tuple-element.237), channel_id=1, source_target_pairs={{0,8},{8,16},{16,24},{1,9},{9,17},{17,25},{2,10},{10,18},{18,26},{... | collective-permute-start | bytes 15428 | tf_op jit(solution)/shard_map/ppermute | solution.py:24
  5.1 52.9 %collective-permute-start.7 = (f32[1,5,257]{2,1,0:T(8,128)S(1)}, f32[1,5,257]{2,1,0:T(8,128)S(1)}, u32[]{:S(2)}, u32[]{:S(2)}) collective-permute-start(f32[1,5,257]{2,1,0:T(8,128)S(1)} %get-tuple-element.238), channel_id=1, source_target_pairs={{8,0},{16,8},{24,16},{9,1},{17,9},{25,17},{10,2},{18,10},{26,18},{... | collective-permute-start | bytes 15428 | tf_op jit(solution)/shard_map/ppermute | solution.py:26
  9.2 16.8 %collective-permute-start.18 = (f32[1,3,129]{2,1,0:T(4,128)S(1)}, f32[1,3,129]{2,1,0:T(4,128)S(1)}, u32[]{:S(2)}, u32[]{:S(2)}) collective-permute-start(f32[1,3,129]{2,1,0:T(4,128)S(1)} %get-tuple-element.391), channel_id=1, source_target_pairs={{0,8},{8,16},{16,24},{1,9},{9,17},{17,25},{2,10},{10,18},{18,26},{... | collective-permute-start | bytes 4652 | tf_op jit(solution)/shard_map/ppermute | solution.py:24
  11.5 10.1 %collective-permute-start.30 = (f32[1,2,65]{2,1,0:T(2,128)S(1)}, f32[1,2,65]{2,1,0:T(2,128)S(1)}, u32[]{:S(2)}, u32[]{:S(2)}) collective-permute-start(f32[1,2,65]{2,1,0:T(2,128)S(1)} %get-tuple-element.513), channel_id=1, source_target_pairs={{0,8},{8,16},{16,24},{1,9},{9,17},{17,25},{2,10},{10,18},{18,26},{... | collective-permute-start | bytes 1568 | tf_op jit(solution)/shard_map/ppermute | solution.py:24
  13.4 10.6 %collective-permute-start.31 = (f32[1,2,65]{2,1,0:T(2,128)S(1)}, f32[1,2,65]{2,1,0:T(2,128)S(1)}, u32[]{:S(2)}, u32[]{:S(2)}) collective-permute-start(f32[1,2,65]{2,1,0:T(2,128)S(1)} %get-tuple-element.514), channel_id=1, source_target_pairs={{8,0},{16,8},{24,16},{9,1},{17,9},{25,17},{10,2},{18,10},{26,18},{... | collective-permute-start | bytes 1568 | tf_op jit(solution)/shard_map/ppermute | solution.py:26
  21.6 7.9 %collective-permute-start.19 = (f32[1,3,129]{2,1,0:T(4,128)S(1)}, f32[1,3,129]{2,1,0:T(4,128)S(1)}, u32[]{:S(2)}, u32[]{:S(2)}) collective-permute-start(f32[1,3,129]{2,1,0:T(4,128)S(1)} %get-tuple-element.392), channel_id=1, source_target_pairs={{8,0},{16,8},{24,16},{9,1},{17,9},{25,17},{10,2},{18,10},{26,18},{... | collective-permute-start | bytes 4652 | tf_op jit(solution)/shard_map/ppermute | solution.py:26
  24.0 39.8 %collective-permute-start = (f32[1,5,257]{2,1,0:T(8,128)S(1)}, f32[1,5,257]{2,1,0:T(8,128)S(1)}, u32[]{:S(2)}, u32[]{:S(2)}) collective-permute-start(f32[1,5,257]{2,1,0:T(8,128)S(1)} %get-tuple-element.135), channel_id=1, source_target_pairs={{0,8},{8,16},{16,24},{1,9},{9,17},{17,25},{2,10},{10,18},{18,26},{... | collective-permute-start | bytes 15428 | tf_op jit(solution)/shard_map/ppermute | solution.py:24
  36.4 8.1 %collective-permute-start.35 = (f32[4,4,1]{2,1,0:T(4,128)S(1)}, f32[4,4,1]{2,1,0:T(4,128)S(1)}, u32[]{:S(2)}, u32[]{:S(2)}) collective-permute-start(f32[4,4,1]{2,1,0:T(4,128)S(1)} %get-tuple-element.416), channel_id=1, source_target_pairs={{1,0},{3,2},{5,4},{7,6},{9,8},{11,10},{13,12},{15,14},{17,16},{19,... | collective-permute-start | bytes 200 | tf_op jit(solution)/shard_map/ppermute | solution.py:26
  51.3 6.5 %collective-permute-start.23 = (f32[5,5,1]{2,1,0:T(8,128)S(1)}, f32[5,5,1]{2,1,0:T(8,128)S(1)}, u32[]{:S(2)}, u32[]{:S(2)}) collective-permute-start(f32[5,5,1]{2,1,0:T(8,128)S(1)} %get-tuple-element.262), channel_id=1, source_target_pairs={{1,0},{3,2},{5,4},{7,6},{9,8},{11,10},{13,12},{15,14},{17,16},{19,... | collective-permute-start | bytes 308 | tf_op jit(solution)/shard_map/ppermute | solution.py:26
  55.8 8.0 %collective-permute-start.1 = (f32[1,5,257]{2,1,0:T(8,128)S(1)}, f32[1,5,257]{2,1,0:T(8,128)S(1)}, u32[]{:S(2)}, u32[]{:S(2)}) collective-permute-start(f32[1,5,257]{2,1,0:T(8,128)S(1)} %get-tuple-element.136), channel_id=1, source_target_pairs={{8,0},{16,8},{24,16},{9,1},{17,9},{25,17},{10,2},{18,10},{26,18},{... | collective-permute-start | bytes 15428 | tf_op jit(solution)/shard_map/ppermute | solution.py:26
  58.0 11.8 %collective-permute-start.8 = (f32[7,1,257]{2,1,0:T(1,128)S(1)}, f32[7,1,257]{2,1,0:T(1,128)S(1)}, u32[]{:S(2)}, u32[]{:S(2)}) collective-permute-start(f32[7,1,257]{2,1,0:T(1,128)S(1)} %get-tuple-element.147), channel_id=1, source_target_pairs={{0,2},{2,4},{4,6},{1,3},{3,5},{5,7},{8,10},{10,12},{12,14},{9,11},... | collective-permute-start | bytes 21596 | tf_op jit(solution)/shard_map/ppermute | solution.py:24
  59.9 9.8 %collective-permute-start.9 = (f32[7,1,257]{2,1,0:T(1,128)S(1)}, f32[7,1,257]{2,1,0:T(1,128)S(1)}, u32[]{:S(2)}, u32[]{:S(2)}) collective-permute-start(f32[7,1,257]{2,1,0:T(1,128)S(1)} %get-tuple-element.148), channel_id=1, source_target_pairs={{2,0},{4,2},{6,4},{3,1},{5,3},{7,5},{10,8},{12,10},{14,12},{11,9},... | collective-permute-start | bytes 21596 | tf_op jit(solution)/shard_map/ppermute | solution.py:26
  63.9 11.8 %collective-permute-start.2 = (f32[7,1,257]{2,1,0:T(1,128)S(1)}, f32[7,1,257]{2,1,0:T(1,128)S(1)}, u32[]{:S(2)}, u32[]{:S(2)}) collective-permute-start(f32[7,1,257]{2,1,0:T(1,128)S(1)} %get-tuple-element.145), channel_id=1, source_target_pairs={{0,2},{2,4},{4,6},{1,3},{3,5},{5,7},{8,10},{10,12},{12,14},{9,11},... | collective-permute-start | bytes 21596 | tf_op jit(solution)/shard_map/ppermute | solution.py:24
  65.8 9.8 %collective-permute-start.3 = (f32[7,1,257]{2,1,0:T(1,128)S(1)}, f32[7,1,257]{2,1,0:T(1,128)S(1)}, u32[]{:S(2)}, u32[]{:S(2)}) collective-permute-start(f32[7,1,257]{2,1,0:T(1,128)S(1)} %get-tuple-element.146), channel_id=1, source_target_pairs={{2,0},{4,2},{6,4},{3,1},{5,3},{7,5},{10,8},{12,10},{14,12},{11,9},... | collective-permute-start | bytes 21596 | tf_op jit(solution)/shard_map/ppermute | solution.py:26
  69.8 11.8 %collective-permute-start.10 = (f32[7,7,1]{2,1,0:T(8,128)S(1)}, f32[7,7,1]{2,1,0:T(8,128)S(1)}, u32[]{:S(2)}, u32[]{:S(2)}) collective-permute-start(f32[7,7,1]{2,1,0:T(8,128)S(1)} %get-tuple-element.129), channel_id=1, source_target_pairs={{0,1},{2,3},{4,5},{6,7},{8,9},{10,11},{12,13},{14,15},{16,17},{18,... | collective-permute-start | bytes 596 | tf_op jit(solution)/shard_map/ppermute | solution.py:24
  71.1 10.5 %collective-permute-start.11 = (f32[7,7,1]{2,1,0:T(8,128)S(1)}, f32[7,7,1]{2,1,0:T(8,128)S(1)}, u32[]{:S(2)}, u32[]{:S(2)}) collective-permute-start(f32[7,7,1]{2,1,0:T(8,128)S(1)} %get-tuple-element.130), channel_id=1, source_target_pairs={{1,0},{3,2},{5,4},{7,6},{9,8},{11,10},{13,12},{15,14},{17,16},{19,... | collective-permute-start | bytes 596 | tf_op jit(solution)/shard_map/ppermute | solution.py:26
  75.7 6.3 %collective-permute-start.4 = (f32[7,7,1]{2,1,0:T(8,128)S(1)}, f32[7,7,1]{2,1,0:T(8,128)S(1)}, u32[]{:S(2)}, u32[]{:S(2)}) collective-permute-start(f32[7,7,1]{2,1,0:T(8,128)S(1)} %get-tuple-element.127), channel_id=1, source_target_pairs={{0,1},{2,3},{4,5},{6,7},{8,9},{10,11},{12,13},{14,15},{16,17},{18,... | collective-permute-start | bytes 596 | tf_op jit(solution)/shard_map/ppermute | solution.py:24
  77.0 6.1 %collective-permute-start.5 = (f32[7,7,1]{2,1,0:T(8,128)S(1)}, f32[7,7,1]{2,1,0:T(8,128)S(1)}, u32[]{:S(2)}, u32[]{:S(2)}) collective-permute-start(f32[7,7,1]{2,1,0:T(8,128)S(1)} %get-tuple-element.128), channel_id=1, source_target_pairs={{1,0},{3,2},{5,4},{7,6},{9,8},{11,10},{13,12},{15,14},{17,16},{19,... | collective-permute-start | bytes 596 | tf_op jit(solution)/shard_map/ppermute | solution.py:26
  197.8 6.1 %collective-permute-start.53 = (f32[7,7,1]{2,1,0:T(8,128)S(1)}, f32[7,7,1]{2,1,0:T(8,128)S(1)}, u32[]{:S(2)}, u32[]{:S(2)}) collective-permute-start(f32[7,7,1]{2,1,0:T(8,128)S(1)} %get-tuple-element.126), channel_id=1, source_target_pairs={{1,0},{3,2},{5,4},{7,6},{9,8},{11,10},{13,12},{15,14},{17,16},{19,... | collective-permute-start | bytes 596 | tf_op jit(solution)/shard_map/ppermute | solution.py:26
  228.1 6.1 %collective-permute-start.59 = (f32[7,7,1]{2,1,0:T(8,128)S(1)}, f32[7,7,1]{2,1,0:T(8,128)S(1)}, u32[]{:S(2)}, u32[]{:S(2)}) collective-permute-start(f32[7,7,1]{2,1,0:T(8,128)S(1)} %get-tuple-element.124), channel_id=1, source_target_pairs={{1,0},{3,2},{5,4},{7,6},{9,8},{11,10},{13,12},{15,14},{17,16},{19,... | collective-permute-start | bytes 596 | tf_op jit(solution)/shard_map/ppermute | solution.py:26
  270.9 6.5 %collective-permute-start.62 = (f32[5,1,129]{2,1,0:T(1,128)S(1)}, f32[5,1,129]{2,1,0:T(1,128)S(1)}, u32[]{:S(2)}, u32[]{:S(2)}) collective-permute-start(f32[5,1,129]{2,1,0:T(1,128)S(1)} %get-tuple-element.287), channel_id=1, source_target_pairs={{0,2},{2,4},{4,6},{1,3},{3,5},{5,7},{8,10},{10,12},{12,14},{9,11},... | collective-permute-start | bytes 7748 | tf_op jit(solution)/shard_map/ppermute | solution.py:24
  272.8 6.4 %collective-permute-start.63 = (f32[5,1,129]{2,1,0:T(1,128)S(1)}, f32[5,1,129]{2,1,0:T(1,128)S(1)}, u32[]{:S(2)}, u32[]{:S(2)}) collective-permute-start(f32[5,1,129]{2,1,0:T(1,128)S(1)} %get-tuple-element.288), channel_id=1, source_target_pairs={{2,0},{4,2},{6,4},{3,1},{5,3},{7,5},{10,8},{12,10},{14,12},{11,9},... | collective-permute-start | bytes 7748 | tf_op jit(solution)/shard_map/ppermute | solution.py:26
  375.7 6.1 %collective-permute-start.89 = (f32[7,7,1]{2,1,0:T(8,128)S(1)}, f32[7,7,1]{2,1,0:T(8,128)S(1)}, u32[]{:S(2)}, u32[]{:S(2)}) collective-permute-start(f32[7,7,1]{2,1,0:T(8,128)S(1)} %get-tuple-element.122), channel_id=1, source_target_pairs={{1,0},{3,2},{5,4},{7,6},{9,8},{11,10},{13,12},{15,14},{17,16},{19,... | collective-permute-start | bytes 596 | tf_op jit(solution)/shard_map/ppermute | solution.py:26
  405.4 6.1 %collective-permute-start.95 = (f32[7,7,1]{2,1,0:T(8,128)S(1)}, f32[7,7,1]{2,1,0:T(8,128)S(1)}, u32[]{:S(2)}, u32[]{:S(2)}) collective-permute-start(f32[7,7,1]{2,1,0:T(8,128)S(1)} %get-tuple-element.120), channel_id=1, source_target_pairs={{1,0},{3,2},{5,4},{7,6},{9,8},{11,10},{13,12},{15,14},{17,16},{19,... | collective-permute-start | bytes 596 | tf_op jit(solution)/shard_map/ppermute | solution.py:26
  (93 other events, 425.6 us)
